TPU v7x, 32 devices: a whole 2x2x4 slice. The times are simulated.
32 devices in a mesh: row: 2 (over x), col: 4 (over z), layer: 4 (over y, core).
Axes of the slice: x: 2, y: 2, z: 4, core: 2. Of those that a mesh axis runs over, the one named last changes fastest.
Arguments:
- left_factor: float32 [2048, 4096], P('row', ('layer', 'col')), may hold values from 0.01 to 1
- right_factor: float32 [4096, 4096], P(('layer', 'row'), 'col'), may hold values from 0.01 to 1
- left_occupancy: int32 [16, 32], replicated, may hold values 0 or 1
- right_occupancy: int32 [32, 32], replicated, may hold values 0 or 1
Outputs:
- flow: float32 [2048, 4096], P(('row', 'layer'), 'col')
All inputs are finite; a program needn't handle non-finite values.
Results may differ from a plain program's by a relative error of at most 0.000082.
Values sent between devices are 32-bit elements; how exact they have to be, the bound alone decides.
No kernel may reach another device: no remote copies, remote signals or barrier semaphores. Data moves between devices by JAX's collectives and lax.ppermute only.
A program may use at most 64 MiB of HBM per device.

v0:
```python
import jax
import jax.numpy as jnp
from jax import lax
from jax.sharding import PartitionSpec as P

BLOCK = 128
EPSILON = 1e-06


def widen(flags):
    return jnp.repeat(jnp.repeat(flags.astype(jnp.float32), BLOCK, 0), BLOCK, 1)


def on_device(left_factor, right_factor, left_occupancy, right_occupancy):
    row_index = lax.axis_index("row")
    col_index = lax.axis_index("col")
    layer_index = lax.axis_index("layer")
    right_whole = lax.all_gather(right_factor, "row", axis=0, tiled=True)
    depth = right_whole.shape[0]
    width = right_whole.shape[1]
    depth_blocks = depth // BLOCK
    width_blocks = width // BLOCK
    right_flags = lax.dynamic_slice(
        right_occupancy,
        (layer_index * depth_blocks, col_index * width_blocks),
        (depth_blocks, width_blocks),
    )
    right_masked = right_whole * widen(right_flags)
    band_rows = left_factor.shape[0]
    row_blocks = band_rows // BLOCK
    left_flags = lax.dynamic_slice(
        left_occupancy,
        (row_index * row_blocks, layer_index * depth_blocks),
        (row_blocks, depth_blocks),
    )
    left_mask = widen(left_flags)
    left_whole = lax.all_gather(left_factor, "col", axis=1, tiled=True)
    left_masked = left_whole * left_mask
    owned = lax.psum_scatter(
        jnp.dot(
            left_masked,
            right_masked,
            precision=lax.Precision.HIGHEST,
            preferred_element_type=jnp.float32,
        ),
        "layer",
        scatter_dimension=0,
        tiled=True,
    )
    squared = owned * owned
    totals = lax.psum(jnp.sum(squared, axis=0), ("row", "layer"))
    total_rows = band_rows * lax.axis_size("row")
    return total_rows * squared / (totals + EPSILON)


def solution(mesh):
    return jax.shard_map(
        on_device,
        mesh=mesh,
        in_specs=(P("row", ("layer", "col")), P(("layer", "row"), "col"), P(), P()),
        out_specs=P(("row", "layer"), "col"),
        check_vma=False,
    )
```

profile of v0, /device:TPU:0, one launch (start us, length us, event | category | flops | bytes accessed | tf_op | source)
XLA Modules:
  0.0 237.0 jit_solution(607008218345202250)
XLA Ops:
  6.5 0.0 all-gather.5.cloned.1.call-start
  6.5 0.7 all-gather.5.cloned.1.call-update
  7.3 0.0 all-gather.3.cloned.1.call-start
  7.3 0.7 all-gather.3.cloned.1.call-update
  8.0 0.0 reduce-scatter.2.cloned.1.call-start
  8.1 0.8 dynamic-slice_convert_fusion
  8.8 59.5 %all-gather.5.cloned.1.call-done = f32[1024,1024]{1,0:T(8,128)} async-done(((f32[512,1024]{1,0:T(8,128)}), f32[1024,1024]{1,0:T(8,128)}) %all-gather.5.cloned.1.call-update) | async-done | bytes 4194320 | tf_op jit(solution)/shard_map/all_gather | solution.py:18
  68.4 82.3 %all-gather.3.cloned.1.call-done = f32[1024,1024]{1,0:T(8,128)} async-done(((f32[1024,256]{1,0:T(8,128)}), f32[1024,1024]{1,0:T(8,128)}) %all-gather.3.cloned.1.call-update) | async-done | bytes 4194320 | tf_op jit(solution)/shard_map/all_gather | solution.py:37
  150.7 0.0 copy-start
  150.7 0.0 copy-start.1
  150.8 1.1 broadcast_in_dim.14
  151.9 1.1 broadcast_in_dim.16
  153.1 0.0 copy-done
  153.1 1.1 copy-done.1
  154.2 16.8 %fusion = f32[1024,1024]{1,0:T(8,128)} fusion(f32[1024,1024]{1,0:T(8,128)S(1)} %copy-done, f32[128,8,8,128]{3,2,1,0:T(8,128)S(1)} %bitcast.11, f32[1024,1024]{1,0:T(8,128)S(1)} %copy-done.1, f32[128,8,8,128]{3,2,1,0:T(8,128)S(1)} %bitcast.10), kind=kOutput, calls=%fused_computation.1 | convolution fusion | flops 12886999040 | bytes 20971520 | tf_op jit(solution)/shard_map/dot_general | solution.py:40
  171.0 0.0 reduce-scatter.2.cloned.1.call-update
  171.0 43.2 %reduce-scatter.2.cloned.1.call-done = f32[256,1024]{1,0:T(8,128)} async-done(((f32[1024,1024]{1,0:T(8,128)}), f32[256,1024]{1,0:T(8,128)}) %reduce-scatter.2.cloned.1.call-update) | async-done | bytes 1048592 | tf_op jit(solution)/shard_map/reduce_scatter | solution.py:39
  214.3 1.3 multiply_reduce_fusion
  215.6 12.5 %psum.7 = f32[1024]{0:T(1024)S(1)} all-reduce(f32[1024]{0:T(1024)S(1)} %multiply_reduce_fusion), channel_id=1, replica_groups=mesh['row'=2,'col'=4,'layer'=4] {'row','layer'}, use_global_device_ids=true, to_apply=%region_2.0 | all-reduce | flops 1024 | bytes 8192 | tf_op jit(solution)/shard_map/psum | solution.py:51
  228.1 2.4 multiply_divide_fusion
  (3 shorter events, 0.1 us)
Async XLA Ops:
  6.5 61.8 %all-gather.5.cloned.1.call-start = ((), (), s32[]{:S(2)}) async-start(), calls=%async_computation.2 | async-start | bytes 6291456 | tf_op jit(solution)/shard_map/all_gather | solution.py:18
  7.3 143.4 %all-gather.3.cloned.1.call-start = ((), (), s32[]{:S(2)}) async-start(), calls=%async_computation.1 | async-start | bytes 5242880 | tf_op jit(solution)/shard_map/all_gather | solution.py:37
  8.0 206.3 %reduce-scatter.2.cloned.1.call-start = ((), (), s32[]{:S(2)}) async-start(), calls=%async_computation.3 | async-start | bytes 5242880 | tf_op jit(solution)/shard_map/reduce_scatter | solution.py:39
  150.7 2.3 copy-start
  150.7 3.5 %copy-start.1 = (f32[1024,1024]{1,0:T(8,128)S(1)}, f32[1024,1024]{1,0:T(8,128)}, u32[]{:S(2)}) copy-start(f32[1024,1024]{1,0:T(8,128)} %all-gather.3.cloned.1.call-done) | copy-start | bytes 12582916
Sparse Core Ops, SparseCore 0:
  8.9 59.4 all-gather.4
  69.9 80.7 all-gather.2
  171.2 43.0 reduce-scatter.1
where the time goes:
time: 237 us
  waiting for transfers between devices  186 us (78%)
  matrix products  16.8 us (7%)
  between operations  13.2 us (6%)
  blocking collectives  12.5 us (5%)
  other arithmetic  4.48 us (2%)
  local copies, waits for them, and re-layouts  3.47 us (1%)
    all_gather x1, waiting for transfers between devices, on_device(): left_whole = lax.all_gather(left_factor, 'col', axis=1, tiled=True)  82.3 us
    all_gather x1, waiting for transfers between devices, on_device(): right_whole = lax.all_gather(right_factor, 'row', axis=0, tiled=True)  59.5 us
    reduce_scatter x1, waiting for transfers between devices, on_device(): lax.psum_scatter(jnp.dot(left_masked, right_masked, precision=lax.Precisi...  43.2 us
    dot_general x1, matrix products, on_device(): jnp.dot(left_masked, right_masked, precision=lax.Precision.HIGHEST, prefe...  16.8 us
    psum x1, blocking collectives, on_device(): totals = lax.psum(jnp.sum(squared, axis=0), ('row', 'layer'))  12.5 us
  transfers between devices with their start and end apart: 3, of which 3 were waited for; matrix products, arithmetic and copies ran while one was open for 0% of the time, Pallas kernels for 0%

commit v1 on v0

--- a/solution.py
+++ b/solution.py
@@ -34,7 +34,14 @@
         (row_blocks, depth_blocks),
     )
     left_mask = widen(left_flags)
-    left_whole = lax.all_gather(left_factor, "col", axis=1, tiled=True)
+    n_dev = lax.axis_size("col")
+    right = [(i, (i + 1) % n_dev) for i in range(n_dev)]
+    parts = [left_factor]
+    for far in range(1, n_dev):
+        parts = [lax.ppermute(parts[0], "col", right), *parts]
+    whole = jnp.concatenate(parts, axis=1)
+    shift = (lax.axis_index("col") + 1) * parts[-1].shape[1]
+    left_whole = jnp.roll(whole, shift, axis=1)
     left_masked = left_whole * left_mask
     owned = lax.psum_scatter(
         jnp.dot(

time: 237 us -> 184 us (0.78)
  waiting for transfers between devices: 186 us -> 119 us
  local copies, waits for them, and re-layouts: 3.47 us -> 13.8 us
  starting transfers between devices: 0.08 us -> 3.1 us
    all_gather x1 -> x0, waiting for transfers between devices: 82.3 us -> none  [on_device(): left_whole = lax.all_gather(left_factor, 'col', axis=1, tiled=True)]
    ppermute x0 -> x3, waiting for transfers between devices: none -> 76.1 us  [on_device(): parts = [lax.ppermute(parts[0], 'col', right), *parts]]
    all_gather x1, waiting for transfers between devices: 59.5 us -> 0.01 us  [on_device(): right_whole = lax.all_gather(right_factor, 'row', axis=0, tiled=True)]
    unnamed x4 -> x11, local copies, waits for them, and re-layouts: 1.12 us -> 10.4 us
    ppermute x0 -> x3, starting transfers between devices: none -> 3.06 us  [on_device(): parts = [lax.ppermute(parts[0], 'col', right), *parts]]
  transfers between devices with their start and end apart: 3 -> 5, of which waited for: 3 -> 4; matrix products, arithmetic and copies ran while one was open for 0% -> 7% of each run, Pallas kernels for 0% -> 0%
where the time goes in v1:
time: 184 us
  waiting for transfers between devices  119 us (65%)
  matrix products  17.9 us (10%)
  local copies, waits for them, and re-layouts  13.8 us (8%)
  between operations  13.4 us (7%)
  blocking collectives  12.5 us (7%)
  other arithmetic  4.47 us (2%)
  starting transfers between devices  3.1 us (2%)
    ppermute x3, waiting for transfers between devices, on_device(): parts = [lax.ppermute(parts[0], 'col', right), *parts]  76.1 us
    reduce_scatter x1, waiting for transfers between devices, on_device(): lax.psum_scatter(jnp.dot(left_masked, right_masked, precision=lax.Precisi...  42.7 us
    dot_general x1, matrix products, on_device(): jnp.dot(left_masked, right_masked, precision=lax.Precision.HIGHEST, prefe...  17.9 us
    psum x1, blocking collectives, on_device(): totals = lax.psum(jnp.sum(squared, axis=0), ('row', 'layer'))  12.5 us
    unnamed x11, local copies, waits for them, and re-layouts  10.4 us
  transfers between devices with their start and end apart: 5, of which 4 were waited for; matrix products, arithmetic and copies ran while one was open for 7% of the time, Pallas kernels for 0%

profile of v1, /device:TPU:0, one launch (start us, length us, event | category | flops | bytes accessed | tf_op | source)
XLA Modules:
  0.0 184.1 jit_solution(4659363931010956685)
XLA Ops:
  6.5 3.1 %collective-permute-start = (f32[1024,256]{1,0:T(8,128)}, f32[1024,256]{1,0:T(8,128)S(1)}, u32[]{:S(2)}, u32[]{:S(2)}) collective-permute-start(f32[1024,256]{1,0:T(8,128)} %param.4), channel_id=1, source_target_pairs={{0,4},{4,8},{8,12},{12,0},{1,5},{5,9},{9,13},{13,1},{2,6},{6,10},{... | collective-permute-start | bytes 3145736 | tf_op jit(solution)/shard_map/ppermute | solution.py:41
  9.6 0.0 all-gather.2.cloned.1.call-update
  9.6 0.0 reduce-scatter.2.cloned.1.call-start
  9.7 25.4 %collective-permute-done = f32[1024,256]{1,0:T(8,128)S(1)} collective-permute-done((f32[1024,256]{1,0:T(8,128)}, f32[1024,256]{1,0:T(8,128)S(1)}, u32[]{:S(2)}, u32[]{:S(2)}) %collective-permute-start) | collective-permute-done | bytes 1048608 | tf_op jit(solution)/shard_map/ppermute | solution.py:41
  35.1 0.0 collective-permute-start.1
  35.1 26.1 %collective-permute-done.1 = f32[1024,256]{1,0:T(8,128)S(1)} collective-permute-done((f32[1024,256]{1,0:T(8,128)S(1)}, f32[1024,256]{1,0:T(8,128)S(1)}, u32[]{:S(2)}, u32[]{:S(2)}) %collective-permute-start.1) | collective-permute-done | bytes 1048608 | tf_op jit(solution)/shard_map/ppermute | solution.py:41
  61.2 0.8 dynamic-slice_convert_fusion
  62.0 24.6 %collective-permute-done.2 = f32[1024,256]{1,0:T(8,128)} collective-permute-done((f32[1024,256]{1,0:T(8,128)S(1)}, f32[1024,256]{1,0:T(8,128)}, u32[]{:S(2)}, u32[]{:S(2)}) %collective-permute-start.2) | collective-permute-done | bytes 1048608 | tf_op jit(solution)/shard_map/ppermute | solution.py:41
  86.5 2.4 %constant_dynamic-update-slice_fusion.7 = f32[1024,2048]{1,0:T(8,128)} fusion(f32[1024,256]{1,0:T(8,128)} %collective-permute-done.2), kind=kLoop, calls=%fused_computation.15 | loop fusion | bytes 2097152
  88.9 1.1 constant_dynamic-update-slice_fusion.6
  90.1 1.1 constant_dynamic-update-slice_fusion.5
  91.2 1.2 constant_dynamic-update-slice_fusion.4
  92.3 2.4 %constant_dynamic-update-slice_fusion.3 = f32[1024,2048]{1,0:T(8,128)} fusion(f32[1024,2048]{1,0:T(8,128)} %constant_dynamic-update-slice_fusion.4, f32[1024,256]{1,0:T(8,128)} %collective-permute-done.2), kind=kLoop, calls=%fused_computation.11 | loop fusion | bytes 2097152
  94.7 1.1 constant_dynamic-update-slice_fusion.2
  95.8 1.1 constant_dynamic-update-slice_fusion.1
  96.9 1.1 constant_dynamic-update-slice_fusion
  98.1 1.1 broadcast_in_dim.14
  99.3 1.1 broadcast_in_dim.16
  100.4 17.9 %fusion = f32[1024,1024]{1,0:T(8,128)} fusion(f32[1024,1024]{1,0:T(8,128)S(1)} %copy-done.1, f32[128,8,8,128]{3,2,1,0:T(8,128)S(1)} %bitcast.11, f32[128,8,8,128]{3,2,1,0:T(8,128)S(1)} %bitcast.10, f32[1024,2048]{1,0:T(8,128)} %constant_dynamic-update-slice_fusion, s32[]{:T(128)S(6)} %select_n.24), kind=kOutput, calls=%fused_computation.1 | convolution fusion | flops 12886999040 | bytes 20971524 | tf_op jit(solution)/shard_map/dot_general | solution.py:47
  118.3 0.0 reduce-scatter.2.cloned.1.call-update
  118.4 42.7 %reduce-scatter.2.cloned.1.call-done = f32[256,1024]{1,0:T(8,128)} async-done(((f32[1024,1024]{1,0:T(8,128)}), f32[256,1024]{1,0:T(8,128)}) %reduce-scatter.2.cloned.1.call-update) | async-done | bytes 1048592 | tf_op jit(solution)/shard_map/reduce_scatter | solution.py:46
  161.0 1.3 multiply_reduce_fusion
  162.3 12.5 %psum.7 = f32[1024]{0:T(1024)S(1)} all-reduce(f32[1024]{0:T(1024)S(1)} %multiply_reduce_fusion), channel_id=1, replica_groups=mesh['row'=2,'col'=4,'layer'=4] {'row','layer'}, use_global_device_ids=true, to_apply=%region_2.3 | all-reduce | flops 1024 | bytes 8192 | tf_op jit(solution)/shard_map/psum | solution.py:58
  174.9 2.4 %multiply_divide_fusion = f32[256,1024]{1,0:T(8,128)} fusion(f32[256,1024]{1,0:T(8,128)} %reduce-scatter.2.cloned.1.call-done, f32[1024]{0:T(1024)S(1)} %broadcast_add_fusion), kind=kLoop, calls=%fused_computation.6 | loop fusion | flops 786432 | bytes 2101248 | tf_op jit(solution)/shard_map/div | solution.py:60
  (10 shorter events, 0.1 us)
Async XLA Ops:
  6.5 84.7 %copy-start = (f32[1024,256]{1,0:T(8,128)S(1)}, f32[1024,256]{1,0:T(8,128)}, u32[]{:S(2)}) copy-start(f32[1024,256]{1,0:T(8,128)} %param.4) | copy-start | bytes 3145732
  6.5 91.5 %all-gather.2.cloned.1.call-start = ((), (), s32[]{:S(2)}) async-start(), calls=%async_computation.1 | async-start | bytes 6291456 | tf_op jit(solution)/shard_map/all_gather | solution.py:18
  6.5 28.5 %collective-permute-start = (f32[1024,256]{1,0:T(8,128)}, f32[1024,256]{1,0:T(8,128)S(1)}, u32[]{:S(2)}, u32[]{:S(2)}) collective-permute-start(f32[1024,256]{1,0:T(8,128)} %param.4), channel_id=1, source_target_pairs={{0,4},{4,8},{8,12},{12,0},{1,5},{5,9},{9,13},{13,1},{2,6},{6,10},{... | collective-permute-start | bytes 3145736 | tf_op jit(solution)/shard_map/ppermute | solution.py:41
  9.6 151.4 %reduce-scatter.2.cloned.1.call-start = ((), (), s32[]{:S(2)}) async-start(), calls=%async_computation.2 | async-start | bytes 5242880 | tf_op jit(solution)/shard_map/reduce_scatter | solution.py:46
  35.1 26.1 %collective-permute-start.1 = (f32[1024,256]{1,0:T(8,128)S(1)}, f32[1024,256]{1,0:T(8,128)S(1)}, u32[]{:S(2)}, u32[]{:S(2)}) collective-permute-start(f32[1024,256]{1,0:T(8,128)S(1)} %collective-permute-done), channel_id=1, source_target_pairs={{0,4},{4,8},{8,12},{12,0},{1,5},{5,9},{9,13},{13,1},{2,6},{6,10},{... | collective-permute-start | bytes 3145736 | tf_op jit(solution)/shard_map/ppermute | solution.py:41
  61.2 25.4 %collective-permute-start.2 = (f32[1024,256]{1,0:T(8,128)S(1)}, f32[1024,256]{1,0:T(8,128)}, u32[]{:S(2)}, u32[]{:S(2)}) collective-permute-start(f32[1024,256]{1,0:T(8,128)S(1)} %collective-permute-done.1), channel_id=1, source_target_pairs={{0,4},{4,8},{8,12},{12,0},{1,5},{5,9},{9,13},{13,1},{2,6},{6,10},{... | collective-permute-start | bytes 3145736 | tf_op jit(solution)/shard_map/ppermute | solution.py:41
  98.0 2.4 %copy-start.1 = (f32[1024,1024]{1,0:T(8,128)S(1)}, f32[1024,1024]{1,0:T(8,128)}, u32[]{:S(2)}) copy-start(f32[1024,1024]{1,0:T(8,128)} %all-gather.2.cloned.1.call-done) | copy-start | bytes 12582916
Sparse Core Ops, SparseCore 0:
  9.7 58.5 all-gather.1
  118.5 42.4 reduce-scatter.1
